TPU v7x, 128 devices: a whole 4x4x4 slice. The times are simulated.
128 devices in a mesh: rep: 8 (over x_lo, z), fsdp: 16 (over y, x_hi, core).
Axes of the slice: x: 4 (x_hi: 2, x_lo: 2; x = x_hi * 2 + x_lo), y: 4, z: 4, core: 2. Of those that a mesh axis runs over, the one named last changes fastest.
Arguments:
- hidden: bfloat16 [32768, 7168], P(('rep', 'fsdp')), may hold values from -24 to 24
- out_grad: bfloat16 [32768, 2048], P(('rep', 'fsdp')), may hold values from -0.09375 to 0.09375
- inner_params: float32 [8, 7168, 2048], P('rep', 'fsdp'), may hold values from -0.132 to 0.132
- first_moment: bfloat16 [8, 7168, 2048], P('rep', 'fsdp'), may hold values from -6 to 6
- second_moment: bfloat16 [8, 7168, 2048], P('rep', 'fsdp'), may hold values from 0.049804688 to 2
- outer_params: float32 [7168, 2048], P('fsdp', 'rep'), may hold values from -0.12 to 0.12
- outer_momentum: float32 [7168, 2048], P('fsdp', 'rep'), may hold values from -0.012 to 0.012
Outputs:
- new_params: float32 [7168, 2048], P('fsdp')
- new_momentum: float32 [7168, 2048], P('fsdp', 'rep')
- new_first: bfloat16 [8, 7168, 2048], P('rep', 'fsdp')
- new_second: bfloat16 [8, 7168, 2048], P('rep', 'fsdp')
All inputs are finite; a program needn't handle non-finite values.
Results may differ from a plain program's by a relative error of at most 0.009.
Values may be sent and summed in bfloat16 or wider, within the bound.
A program may use at most 192 MiB of HBM per device.

v0:
```python
import jax
import jax.numpy as jnp
from jax import lax
from jax.sharding import PartitionSpec as P

INNER_STEP = 500


beta_one = 0.9
beta_two = 0.95
epsilon = 1e-08
inner_rate = 0.0004
weight_decay = 0.1
outer_rate = 0.7
nesterov = 0.9


def split_up(array, dim, devices):
    before, after = (array.shape[:dim], array.shape[dim + 1 :])
    return jnp.moveaxis(array.reshape(*before, devices, -1, *after), dim, 0)


def sum_at_owner(array, axis, dim):
    tiles = split_up(array, dim, lax.axis_size(axis))
    arrived = lax.all_to_all(tiles, axis, split_axis=0, concat_axis=0, tiled=True)
    return arrived.sum(axis=0)


def per_device(
    hidden, out_grad, inner_params, first_moment, second_moment, outer_params, outer_momentum
):
    shard_rows = inner_params.shape[1]
    token_count = hidden.shape[0]
    columns = lax.all_to_all(hidden, "fsdp", split_axis=1, concat_axis=0, tiled=True)
    segment = lax.all_gather(out_grad, "fsdp", axis=0, tiled=True)
    blocks = segment.shape[0] // token_count
    partial_value = jnp.einsum(
        "btf,btd->bfd",
        columns.reshape(blocks, token_count, shard_rows),
        segment.reshape(blocks, token_count, segment.shape[1]),
        preferred_element_type=jnp.float32,
    )
    rounded = lax.optimization_barrier(partial_value.astype(jnp.bfloat16)).astype(jnp.float32)
    gradient = jnp.sum(rounded, axis=0)
    stacked = gradient[None]
    moment_one = beta_one * first_moment.astype(jnp.float32) + (1.0 - beta_one) * stacked
    moment_two = beta_two * second_moment.astype(jnp.float32) + (1.0 - beta_two) * stacked * stacked
    corrected_one = moment_one / (1.0 - beta_one**INNER_STEP)
    corrected_two = moment_two / (1.0 - beta_two**INNER_STEP)
    stepped = inner_params - inner_rate * (
        corrected_one / (jnp.sqrt(corrected_two) + epsilon) + weight_decay * inner_params
    )
    summed = sum_at_owner(stepped[0], "rep", 1)
    outer_delta = outer_params - summed / lax.axis_size("rep")
    new_momentum = nesterov * outer_momentum + outer_delta
    updated = outer_params - outer_rate * (outer_delta + nesterov * new_momentum)
    gathered = lax.all_gather(updated, "rep", axis=1, tiled=True)
    return (
        gathered,
        new_momentum,
        moment_one.astype(jnp.bfloat16),
        moment_two.astype(jnp.bfloat16),
    )


def solution(mesh):
    return jax.shard_map(
        per_device,
        mesh=mesh,
        in_specs=(
            P(("rep", "fsdp"), None),
            P(("rep", "fsdp"), None),
            P("rep", "fsdp", None),
            P("rep", "fsdp", None),
            P("rep", "fsdp", None),
            P("fsdp", "rep"),
            P("fsdp", "rep"),
        ),
        out_specs=(
            P("fsdp", None),
            P("fsdp", "rep"),
            P("rep", "fsdp", None),
            P("rep", "fsdp", None),
        ),
        check_vma=False,
    )
```

profile of v0, /device:TPU:0, one launch (start us, length us, event | category | flops | bytes accessed | tf_op | source)
XLA Modules:
  0.0 304.4 jit_solution(7644263598147971197)
XLA Ops:
  7.2 0.0 all-gather.3.cloned.1.call-start
  7.2 0.7 all-gather.3.cloned.1.call-update
  7.9 0.0 all-gather.5.cloned.1.call-start
  7.9 5.9 %copy.13 = bf16[256,7168]{0,1:T(8,128)(2,1)} copy(bf16[256,7168]{1,0:T(8,128)(2,1)} %param.7) | data formatting | bytes 7340032 | tf_op args[0]
  13.9 67.3 %all_to_all.21 = bf16[256,16,448]{0,2,1:T(8,128)(2,1)} all-to-all(bf16[256,16,448]{0,2,1:T(8,128)(2,1)} %bitcast.26), channel_id=1, replica_groups=mesh['rep'=8,'fsdp'=16] {'fsdp'}, dimensions={1} | all-to-all | bytes 7340032 | tf_op jit(solution)/shard_map/all_to_all | solution.py:34
  81.1 74.6 %all-gather.3.cloned.1.call-done = bf16[4096,2048]{1,0:T(8,128)(2,1)} async-done(((bf16[256,2048]{1,0:T(8,128)(2,1)}), bf16[4096,2048]{1,0:T(8,128)(2,1)}) %all-gather.3.cloned.1.call-update) | async-done | bytes 16777232 | tf_op jit(solution)/shard_map/all_gather | solution.py:35
  155.7 19.6 %convolution_convert_fusion = bf16[16,448,2048]{2,1,0:T(8,128)(2,1)} fusion(bf16[16,256,2048]{2,1,0:T(8,128)(2,1)} %bitcast.24, bf16[256,16,448]{0,2,1:T(8,128)(2,1)} %all_to_all.21), kind=kOutput, calls=%fused_computation.1 | convolution fusion | flops 7530872832 | bytes 49807360 | tf_op jit(solution)/shard_map/btf,btd->bfd/dot_general | solution.py:37
  175.4 0.0 copy-start
  175.4 12.3 %convert_reduce_fusion = f32[448,2048]{1,0:T(8,128)} fusion(bf16[16,448,2048]{2,1,0:T(8,128)(2,1)} %convolution_convert_fusion), kind=kLoop, calls=%fused_computation | loop fusion | flops 28442624 | bytes 33030144 | tf_op jit(solution)/shard_map/reduce_sum | solution.py:44
  187.7 0.0 copy-done
  187.7 6.4 %fusion.4 = (bf16[1,448,2048]{2,1,0:T(8,128)(2,1)}, f32[1,448,2048]{2,1,0:T(8,128)S(1)}, bf16[1,448,2048]{2,1,0:T(8,128)(2,1)}) fusion(f32[448,2048]{1,0:T(8,128)} %convert_reduce_fusion, bf16[1,448,2048]{2,1,0:T(8,128)(2,1)S(1)} %copy-done, f32[1,448,2048]{2,1,0:T(8,128)} %param.9, bf16[1,448,2048]{2,1,0:T(8,128)(2,1)} %param.10), kind=kLoop, calls=%fused_computation.9 | loop fusion | flops 15597568 | bytes 18350080 | tf_op jit(solution)/shard_map/convert_element_type | solution.py:62
  194.0 1.7 copy.15
  195.7 1.2 copy.14
  196.9 48.5 %all_to_all.22 = f32[8,448,256]{2,1,0:T(8,128)} all-to-all(f32[8,448,256]{2,1,0:T(8,128)S(1)} %copy.14), channel_id=1, replica_groups=mesh['rep'=8,'fsdp'=16] {'rep'}, dimensions={0} | all-to-all | bytes 7340032 | tf_op jit(solution)/shard_map/all_to_all | solution.py:25
  245.4 0.0 copy-start.1
  245.4 0.0 copy-start.2
  245.4 2.4 reduce_sum.22
  247.8 0.0 copy-done.1
  247.8 0.0 copy-done.2
  247.8 1.0 multiply_subtract_fusion.1
  248.9 0.0 all-gather.5.cloned.1.call-update
  248.9 44.4 %all-gather.5.cloned.1.call-done = f32[448,2048]{1,0:T(8,128)} async-done(((f32[448,256]{1,0:T(8,128)}), f32[448,2048]{1,0:T(8,128)}) %all-gather.5.cloned.1.call-update) | async-done | bytes 3670032 | tf_op jit(solution)/shard_map/all_gather | solution.py:57
  293.3 4.3 %copy.17 = f32[448,2048]{1,0:T(8,128)} copy(f32[448,2048]{1,0:T(8,128)} %all-gather.5.cloned.1.call-done) | data formatting | bytes 7340032
Async XLA Ops:
  7.2 148.6 %all-gather.3.cloned.1.call-start = ((), (), s32[]{:S(2)}) async-start(), calls=%async_computation.2 | async-start | bytes 17825792 | tf_op jit(solution)/shard_map/all_gather | solution.py:35
  7.9 285.4 %all-gather.5.cloned.1.call-start = ((), (), s32[]{:S(2)}) async-start(), calls=%async_computation.3 | async-start | bytes 4128768 | tf_op jit(solution)/shard_map/all_gather | solution.py:57
  175.4 12.3 %copy-start = (bf16[1,448,2048]{2,1,0:T(8,128)(2,1)S(1)}, bf16[1,448,2048]{2,1,0:T(8,128)(2,1)}, u32[]{:S(2)}) copy-start(bf16[1,448,2048]{2,1,0:T(8,128)(2,1)} %param.11) | copy-start | bytes 5505028
  245.4 2.4 copy-start.1
  245.4 2.4 copy-start.2
Sparse Core Ops, SparseCore 0:
  10.4 145.2 all-gather.2
  249.0 44.2 all-gather.4
where the time goes:
time: 305 us; the launch traced here: 304 us
  waiting for transfers between devices  120 us (39%)
  blocking collectives  116 us (38%)
  other arithmetic  22.1 us (7%)
  matrix products  19.6 us (6%)
  between operations  14.1 us (5%)
  local copies, waits for them, and re-layouts  13.1 us (4%)
    all_gather x1, waiting for transfers between devices, per_device(): segment = lax.all_gather(out_grad, 'fsdp', axis=0, tiled=True)  74.6 us
    all_to_all x1, blocking collectives, per_device(): lax.all_to_all(hidden, 'fsdp', split_axis=1, concat_axis=0, tiled=True)  67.3 us
    all_to_all x1, blocking collectives, sum_at_owner(): lax.all_to_all(tiles, axis, split_axis=0, concat_axis=0, tiled=True)  48.5 us
    all_gather x1, waiting for transfers between devices, per_device(): gathered = lax.all_gather(updated, 'rep', axis=1, tiled=True)  44.4 us
    dot_general x1, matrix products, per_device(): jnp.einsum('btf,btd->bfd', columns.reshape(blocks, token_count, shard_row...  19.6 us
    reduce_sum x1, other arithmetic, per_device(): gradient = jnp.sum(rounded, axis=0)  12.3 us
    unnamed x9, local copies, waits for them, and re-layouts  11.9 us
    convert_element_type x1, other arithmetic, per_device(): moment_two.astype(jnp.bfloat16)  6.38 us
  transfers between devices with their start and end apart: 2, of which 2 were waited for; matrix products, arithmetic and copies ran while one was open for 2% of the time, Pallas kernels for 0%

commit v1 on v0

v1 whole, which is shorter than its diff:
```python
import functools

import jax
import jax.numpy as jnp
from jax import lax
from jax.experimental import pallas as pl
from jax.experimental.pallas import tpu as pltpu
from jax.sharding import PartitionSpec as P

INNER_STEP = 500

beta_one = 0.9
beta_two = 0.95
epsilon = 1e-08
inner_rate = 0.0004
weight_decay = 0.1
outer_rate = 0.7
nesterov = 0.9

MESH = pl.DeviceIdType.MESH
BF16, F32 = jnp.bfloat16, jnp.float32

CUTS = (112, 112)
OFFS = tuple(sum(CUTS[:p]) for p in range(len(CUTS)))
ORDER = ((0, 0), (1, 0), (0, 1), (1, 1), (0, 2), (1, 2), (0, 3), (1, 3))
PIPES = len(CUTS)
ROWS, COLS, TOK, REP, YS = 448, 2048, 256, 8, 4
HALF = ROWS // 2
OWN = COLS // REP
PEERS = tuple((dx, dz) for dx in range(2) for dz in range(4) if (dx, dz) != (0, 0))


def rem(a, b):
    return lax.rem(a, jnp.int32(b))


def div(a, b):
    return lax.div(a, jnp.int32(b))


def kernel(
    hid, og, ip, fm, sm, op, om,
    o_np, o_nm, o_nf, o_ns,
    hv, hs, hg, ogg, ysend, yrecv, ipv, fmv, smv, opv, omv, stp, rsb, agb,
    ld, ldh, stq, ogs, ogr, hss, hsr, yss, ysr, rss, rsr, ags, agr,
):
    r, f = lax.axis_index("rep"), lax.axis_index("fsdp")
    xl, z = div(r, 4), rem(r, 4)
    y, xh, c = div(f, 4), rem(div(f, 2), 2), rem(f, 2)

    def at(yy, xx, cc):
        return (r, yy * 4 + xx * 2 + cc)

    mate, opp, opp_mate = at(y, xh, 1 - c), at(y, 1 - xh, c), at(y, 1 - xh, 1 - c)
    targets = (mate, opp, opp_mate)
    up, down = at(rem(y + 1, 4), xh, c), at(rem(y + 3, 4), xh, c)

    def peer_rep(dx, dz):
        return rem(xl + dx, 2) * 4 + rem(z + dz, 4)

    def slot(dx, dz):
        return PEERS.index((dx, dz % 4))

    def chunk_cols(s, xx):
        yy = rem(y + 3 - s + 4, 4)
        return pl.multiple_of((yy * 2 + xx) * 896, 128)

    def send(src, dst, ss, rs, to):
        return pltpu.make_async_remote_copy(
            src_ref=src, dst_ref=dst, send_sem=ss, recv_sem=rs, device_id=to, device_id_type=MESH
        )

    og_in = pltpu.make_async_copy(og, ogg.at[pl.ds(0, TOK)], ld.at[0])
    og_in.start()
    chunk_order = tuple((s, o) for o in (1, 0) for s in (0, 2, 1, 3))
    loads = {}
    for i, (s, o) in enumerate(chunk_order):
        xx = rem(xh + o, 2)
        loads[s, o] = pltpu.make_async_copy(
            hid.at[:, pl.ds(chunk_cols(s, xx), 896)], hv.at[i], ldh.at[i]
        )
        loads[s, o].start()
    state_in = [
        pltpu.make_async_copy(a, b, ld.at[1 + i])
        for i, (a, b) in enumerate(((fm.at[0], fmv), (sm.at[0], smv), (ip.at[0], ipv), (op, opv), (om, omv)))
    ]
    for q in state_in:
        q.start()

    barrier = pltpu.get_barrier_semaphore()
    friends = list(targets) + [up, down] + [(peer_rep(dx, dz), f) for dx, dz in PEERS]
    for d in friends:
        pl.semaphore_signal(barrier, inc=1, device_id=d, device_id_type=MESH)
    pl.semaphore_wait(barrier, len(friends))

    og_in.wait()
    own_og = ogg.at[pl.ds(0, TOK)]
    og_x = send(own_og, ogg.at[pl.ds(2 * TOK, TOK)], ogs.at[1], ogr.at[1], opp)
    og_d = send(own_og, ogg.at[pl.ds(TOK, TOK)], ogs.at[0], ogr.at[0], mate)
    og_f = send(
        ogg.at[pl.ds(2 * TOK, TOK)], ogg.at[pl.ds(3 * TOK, TOK)], ogs.at[2], ogr.at[2], mate
    )
    og_x.start()
    og_d.start()

    for i, (s, o) in enumerate(chunk_order):
        loads[s, o].wait()
        turned = hv[i].T
        s_down = (2 - s) % 4
        for p in range(PIPES):
            m, off = CUTS[p], OFFS[p]
            for cc in range(2):
                top = turned[448 * cc + off : 448 * cc + off + m]
                low = turned[448 * cc + HALF + off : 448 * cc + HALF + off + m]
                same = c == cc

                def put(t_same, t_other):
                    for t, cond in ((t_same, same), (t_other, jnp.logical_not(same))):

                        @pl.when(cond)
                        def _(t=t):
                            if t is None:
                                hg[s, 2 * off : 2 * off + m, 0:TOK] = top
                                hg[s_down, 2 * off + m : 2 * off + 2 * m, 0:TOK] = low
                            else:
                                hs[t, s, 2 * off : 2 * off + m, :] = top
                                hs[t, s_down, 2 * off + m : 2 * off + 2 * m, :] = low

                if o:
                    put(1, 2)
                else:
                    put(None, 0)

    hid_copies = {}
    for p, s in ORDER:
        rows = pl.ds(2 * OFFS[p], 2 * CUTS[p])
        for t in (1, 2, 0):
            q = send(
                hs.at[t, s, rows],
                hg.at[s, rows, pl.ds(TOK * (t + 1), TOK)],
                hss.at[p, s, t], hsr.at[p, s, t], targets[t],
            )
            q.start()
            hid_copies[p, s, t] = q

    og_d.wait_recv()
    og_x.wait_recv()
    og_f.start()
    og_f.wait_recv()

    y_copies, rs_copies, ag_copies = {}, {}, {}
    loaded = False

    def partial(p, s, n):
        rows = slice(2 * OFFS[p], 2 * OFFS[p] + 2 * CUTS[p])
        cols = pl.ds(pl.multiple_of(n * OWN, OWN), OWN)
        got = jnp.dot(hg[s, rows, :], ogg[:, cols], preferred_element_type=F32)
        if s:
            got = got + yrecv[s - 1, rows, cols].astype(F32)
        return got

    for p, s in ORDER:
        m, off = CUTS[p], OFFS[p]
        rows = slice(2 * off, 2 * off + 2 * m)
        for t in range(3):
            hid_copies[p, s, t].wait_recv()
        if s:
            for q in y_copies[p, s - 1]:
                q.wait_recv()
        if s < 3:

            @pl.loop(0, REP)
            def _(n):
                cols = pl.ds(pl.multiple_of(n * OWN, OWN), OWN)
                ysend[s, rows, cols] = partial(p, s, n).astype(BF16)

            y_copies[p, s] = [
                send(
                    ysend.at[s, pl.ds(start, m)], yrecv.at[s, pl.ds(start, m)],
                    yss.at[p, s, i], ysr.at[p, s, i], to,
                )
                for i, (start, to) in enumerate(((2 * off, up), (2 * off + m, down)))
            ]
            for q in y_copies[p, s]:
                q.start()
            continue
        if not loaded:
            for q in state_in:
                q.wait()
            loaded = True

        @pl.loop(0, REP)
        def _(n):
            cols = pl.ds(pl.multiple_of(n * OWN, OWN), OWN)
            gradient = partial(p, s, n)
            for i, start in enumerate((off, HALF + off)):
                g = gradient[i * m : (i + 1) * m]
                at_rows = slice(start, start + m)
                one = beta_one * fmv[at_rows, cols].astype(F32) + (1.0 - beta_one) * g
                two = beta_two * smv[at_rows, cols].astype(F32) + (1.0 - beta_two) * g * g
                fmv[at_rows, cols] = one.astype(BF16)
                smv[at_rows, cols] = two.astype(BF16)
                w = ipv[at_rows, cols]
                hat_one = one * (1.0 / (1.0 - beta_one**INNER_STEP))
                hat_two = two * (1.0 / (1.0 - beta_two**INNER_STEP))
                stp[n, 2 * off + i * m : 2 * off + (i + 1) * m, :] = w - inner_rate * (
                    hat_one / (jnp.sqrt(hat_two) + epsilon) + weight_decay * w
                )

        span = pl.ds(2 * off, 2 * m)
        rs_copies[p] = []
        for dx, dz in PEERS:
            there, k = peer_rep(dx, dz), slot(dx, -dz)
            q = send(stp.at[there, span], rsb.at[k, span], rss.at[p, k], rsr.at[p, k], (there, f))
            q.start()
            rs_copies[p].append(q)

    stores = []
    for j, (a, b) in enumerate(((fmv, o_nf), (smv, o_ns))):
        q = pltpu.make_async_copy(a, b, stq.at[j])
        q.start()
        stores.append(q)

    for p in range(PIPES):
        m, off = CUTS[p], OFFS[p]
        span = pl.ds(2 * off, 2 * m)
        for q in rs_copies[p]:
            q.wait_recv()
        rows = slice(2 * off, 2 * off + 2 * m)
        summed = stp[r, rows, :]
        for k in range(len(PEERS)):
            summed = summed + rsb[k, rows, :]
        for i, start in enumerate((off, HALF + off)):
            at_rows = slice(start, start + m)
            params = opv[at_rows, :]
            delta = params - summed[i * m : (i + 1) * m] / REP
            momentum = nesterov * omv[at_rows, :] + delta
            omv[at_rows, :] = momentum
            agb[r, 2 * off + i * m : 2 * off + (i + 1) * m, :] = (
                params - outer_rate * (delta + nesterov * momentum)
            ).astype(BF16)
        ag_copies[p] = []
        for dx, dz in PEERS:
            there, k = peer_rep(dx, dz), slot(dx, -dz)
            q = send(agb.at[r, span], agb.at[r, span], ags.at[p, k], agr.at[p, k], (there, f))
            q.start()
            ag_copies[p].append(q)

    q = pltpu.make_async_copy(omv, o_nm, stq.at[2])
    q.start()
    stores.append(q)
    for p in range(PIPES):
        m, off = CUTS[p], OFFS[p]
        span = pl.ds(2 * off, 2 * m)
        for q in ag_copies[p]:
            q.wait_recv()
        for k in range(REP):
            for i, start in enumerate((off, HALF + off)):
                q = pltpu.make_async_copy(
                    agb.at[k, pl.ds(2 * off + i * m, m)],
                    o_np.at[pl.ds(start, m), pl.ds(k * OWN, OWN)],
                    stq.at[3 + (p * REP + k) * 2 + i],
                )
                q.start()
                stores.append(q)

    for q in (og_x, og_d, og_f):
        q.wait_send()
    for q in hid_copies.values():
        q.wait_send()
    for group in (y_copies, rs_copies, ag_copies):
        for qs in group.values():
            for q in qs:
                q.wait_send()
    for q in stores:
        q.wait()


def per_device(hidden, out_grad, inner_params, first, second, outer_params, outer_momentum):
    any_ = pl.BlockSpec(memory_space=pl.ANY)
    dma = pltpu.SemaphoreType.DMA
    n = len(PEERS)
    params, momentum, one, two = pl.pallas_call(
        kernel,
        out_shape=(
            jax.ShapeDtypeStruct((ROWS, COLS), BF16),
            jax.ShapeDtypeStruct((ROWS, OWN), F32),
            jax.ShapeDtypeStruct((ROWS, COLS), BF16),
            jax.ShapeDtypeStruct((ROWS, COLS), BF16),
        ),
        in_specs=[any_] * 7,
        out_specs=(any_,) * 4,
        scratch_shapes=[
            pltpu.VMEM((8, TOK, 896), BF16),
            pltpu.VMEM((3, YS, ROWS, TOK), BF16),
            pltpu.VMEM((YS, ROWS, 4 * TOK), BF16),
            pltpu.VMEM((4 * TOK, COLS), BF16),
            pltpu.VMEM((3, ROWS, COLS), BF16),
            pltpu.VMEM((3, ROWS, COLS), BF16),
            pltpu.VMEM((ROWS, COLS), F32),
            pltpu.VMEM((ROWS, COLS), BF16),
            pltpu.VMEM((ROWS, COLS), BF16),
            pltpu.VMEM((ROWS, OWN), F32),
            pltpu.VMEM((ROWS, OWN), F32),
            pltpu.VMEM((REP, ROWS, OWN), F32),
            pltpu.VMEM((n, ROWS, OWN), F32),
            pltpu.VMEM((REP, ROWS, OWN), BF16),
            dma((6,)),
            dma((8,)),
            dma((3 + PIPES * REP * 2,)),
            dma((3,)),
            dma((3,)),
            dma((PIPES, YS, 3)),
            dma((PIPES, YS, 3)),
            dma((PIPES, 3, 2)),
            dma((PIPES, 3, 2)),
            dma((PIPES, n)),
            dma((PIPES, n)),
            dma((PIPES, n)),
            dma((PIPES, n)),
        ],
        compiler_params=pltpu.CompilerParams(
            collective_id=1, has_side_effects=True, vmem_limit_bytes=60_000_000
        ),
        name="step",
    )(hidden, out_grad, inner_params, first, second, outer_params, outer_momentum)
    return params.astype(F32), momentum, one[None], two[None]


def solution(mesh):
    return jax.shard_map(
        per_device,
        mesh=mesh,
        in_specs=(
            P(("rep", "fsdp"), None),
            P(("rep", "fsdp"), None),
            P("rep", "fsdp", None),
            P("rep", "fsdp", None),
            P("rep", "fsdp", None),
            P("fsdp", "rep"),
            P("fsdp", "rep"),
        ),
        out_specs=(
            P("fsdp", None),
            P("fsdp", "rep"),
            P("rep", "fsdp", None),
            P("rep", "fsdp", None),
        ),
        check_vma=False,
    )
```

time: 305 us -> 178 us (0.58)
  Pallas kernels: 0 us -> 167 us
  waiting for transfers between devices: 120 us -> 0 us
  blocking collectives: 116 us -> 0 us
  matrix products: 19.6 us -> 0 us
  other arithmetic: 22.1 us -> 3.93 us
  between operations: 14.1 us -> 0.66 us
  local copies, waits for them, and re-layouts: 13.1 us -> 4.16 us
    pallas_call x0 -> x1, Pallas kernels: none -> 167 us  [per_device(): pl.pallas_call(kernel, out_shape=(jax.ShapeDtypeStruct((ROWS, COLS), BF16...]
    all_gather x2 -> x0, waiting for transfers between devices: 119 us -> none  [the longest x1 74.6 us: per_device(): segment = lax.all_gather(out_grad, 'fsdp', axis=0, tiled=True)]
    all_to_all x2 -> x0, blocking collectives: 116 us -> none  [the longest x1 67.3 us: per_device(): lax.all_to_all(hidden, 'fsdp', split_axis=1, concat_axis=0, tiled=True)]
    dot_general x1 -> x0, matrix products: 19.6 us -> none  [per_device(): jnp.einsum('btf,btd->bfd', columns.reshape(blocks, token_count, shard_row...]
    reduce_sum x2 -> x0, other arithmetic: 14.7 us -> none  [the longest x1 12.3 us: per_device(): gradient = jnp.sum(rounded, axis=0)]
    unnamed x9, local copies, waits for them, and re-layouts: 11.9 us -> 4.16 us
  transfers between devices with their start and end apart: 2 -> 0, of which waited for: 2 -> 0; matrix products, arithmetic and copies ran while one was open for 2% -> 0% of each run, Pallas kernels for 0% -> 0%
where the time goes in v1:
time: 178 us; the launch traced here: 176 us
  Pallas kernels  167 us (94%)
  local copies, waits for them, and re-layouts  4.16 us (2%)
  other arithmetic  3.93 us (2%)
    pallas_call x1, Pallas kernels, per_device(): pl.pallas_call(kernel, out_shape=(jax.ShapeDtypeStruct((ROWS, COLS), BF16...  167 us
    unnamed x9, local copies, waits for them, and re-layouts  4.16 us
    convert_element_type x1, other arithmetic, per_device(): return (params.astype(F32), momentum, one[None], two[None])  3.93 us

profile of v1, /device:TPU:0, one launch (start us, length us, event | category | flops | bytes accessed | tf_op | source)
XLA Modules:
  0.0 175.6 jit_solution(15150357291123150072)
XLA Ops:
  0.6 166.9 %step.1 = (bf16[448,2048]{1,0:T(8,128)(2,1)}, f32[448,256]{1,0:T(8,128)}, bf16[448,2048]{1,0:T(8,128)(2,1)}, bf16[448,2048]{1,0:T(8,128)(2,1)}) custom-call(bf16[256,7168]{1,0:T(8,128)(2,1)} %hid.1, bf16[256,2048]{1,0:T(8,128)(2,1)} %og.1, f32[1,448,2048]{2,1,0:T(8,128)} %ip.1, bf16[1,448,2048]{2,1,0:T(8,128)(2,1)} %fm.1, bf16[1,448,2048]{2,1,0:T(8,128)(2,1)} %sm.1, ...), custom_call_target="tpu_custom_call" | custom-call | tf_op jit(solution)/shard_map/step/pallas_call | solution.py:283
  167.5 0.0 copy-start.2
  167.5 0.0 copy-start.1
  167.5 3.9 %convert_element_type.3 = f32[448,2048]{1,0:T(8,128)} convert(bf16[448,2048]{1,0:T(8,128)(2,1)} %get-tuple-element.8) | non-fusion elementwise | flops 917504 | bytes 5505024 | tf_op jit(solution)/shard_map/convert_element_type | solution.py:327
  171.5 0.0 copy-done.2
  171.5 0.8 copy.14
  172.2 0.0 copy-done.1
  172.2 0.0 copy-start
  172.2 1.2 copy.15
  173.5 0.9 copy-done
  174.4 1.2 copy.16
Async XLA Ops:
  167.5 3.9 %copy-start.2 = (f32[448,256]{1,0:T(8,128)S(1)}, f32[448,256]{1,0:T(8,128)}, u32[]{:S(2)}) copy-start(f32[448,256]{1,0:T(8,128)} %get-tuple-element.17) | copy-start | bytes 1376260
  167.5 4.7 %copy-start.1 = (bf16[448,2048]{1,0:T(8,128)(2,1)S(1)}, bf16[448,2048]{1,0:T(8,128)(2,1)}, u32[]{:S(2)}) copy-start(bf16[448,2048]{1,0:T(8,128)(2,1)} %get-tuple-element.10) | copy-start | bytes 5505028
  172.2 2.2 %copy-start = (bf16[448,2048]{1,0:T(8,128)(2,1)S(1)}, bf16[448,2048]{1,0:T(8,128)(2,1)}, u32[]{:S(2)}) copy-start(bf16[448,2048]{1,0:T(8,128)(2,1)} %get-tuple-element.11) | copy-start | bytes 5505028

commit v2 on v0

v2 whole, which is shorter than its diff:
```python
import functools

import jax
import jax.numpy as jnp
from jax import lax
from jax.experimental import pallas as pl
from jax.experimental.pallas import tpu as pltpu
from jax.sharding import PartitionSpec as P

INNER_STEP = 500

beta_one = 0.9
beta_two = 0.95
epsilon = 1e-08
inner_rate = 0.0004
weight_decay = 0.1
outer_rate = 0.7
nesterov = 0.9

MESH = pl.DeviceIdType.MESH
BF16, F32 = jnp.bfloat16, jnp.float32

CUTS = (64, 64, 16, 32, 16, 32)
OUT = 5
OFFS = tuple(sum(CUTS[:p]) for p in range(len(CUTS)))
PIPES = len(CUTS)
ROWS, COLS, TOK, REP, YS = 448, 2048, 256, 8, 4
HALF = ROWS // 2
OWN = COLS // REP
PARTS = 4
WIDE = COLS // PARTS
LEAVE = (
    (-1, 0), (0, 0), (1, 0), (2, 0), (-1, 1), (-1, 2), (-1, 3), (3, 0), (4, 0), (0, 1), (1, 1), (2, 1), (3, 1),
    (4, 1), (0, 2), (1, 2), (2, 2), (3, 2), (4, 2), (0, 3), (1, 3), (2, 3), (3, 3), (4, 3),
)
TASKS = (
    ("out", 0), ("fwd", 0), ("unit", 0, 0, 0), ("out", 1), ("unit", 2, 0, 0), ("fwd", 1), ("unit", 1, 0, 0),
    ("out", 2), ("unit", 1, 0, 1), ("fwd", 2), ("unit", 1, 0, 2), ("unit", 0, 0, 2), ("unit", 0, 0, 1),
    ("unit", 2, 0, 2), ("fwd", 3), ("out", 3), ("unit", 2, 0, 1), ("unit", 2, 0, 3), ("unit", 0, 0, 3),
    ("unit", 1, 0, 3), ("unit", 3, 0), ("unit", 0, 1), ("unit", 4, 0), ("unit", 1, 1), ("unit", 0, 2),
    ("unit", 3, 1), ("unit", 1, 2), ("adam", 0), ("unit", 4, 1), ("unit", 2, 1), ("inner",), ("adam", 5),
    ("unit", 3, 2), ("adam", 1), ("unit", 4, 2), ("rz", 0), ("unit", 2, 2), ("adam", 3), ("rz", 5), ("adam", 4),
    ("adam", 2), ("rz", 1), ("outer", 0), ("rz", 3), ("rz", 4), ("outer", 5), ("rz", 2), ("outer", 1), ("outer", 3),
    ("outer", 2), ("pass", 5), ("outer", 4), ("pass", 0), ("pass", 1), ("pass", 2), ("pass", 3), ("pass", 4),
    ("end", 1), ("end", 4), ("end", 3), ("end", 5), ("end", 0), ("end", 2),
)
GATHER = "zxxzzx"


def rem(a, b):
    return lax.rem(a, jnp.int32(b))


def div(a, b):
    return lax.div(a, jnp.int32(b))


def kernel(
    hid, og, ip, fm, sm, op, om,
    o_np, o_nm, o_nf, o_ns,
    hv, hs, hg, ogg, acc, ysend, yrecv, ipv, fmv, smv, opv, omv, stp, rsz, xsend, xkeep, xrecv, agb,
    ipr, ips, ipk, hse, hge, ace, yse, yre, xse, xre,
    ld, ldh, stq, ogs, ogm, ogx, ogr, hes, her, yes, yer, xes, xer,
    hss, hsr, yss, ysr, ysp, rzs, rzr, rxs, rxr, axs, axr, azs, azr,
    ips_, ipr_,
):
    scope = jax.named_scope
    r, f = lax.axis_index("rep"), lax.axis_index("fsdp")
    xl, z = div(r, 4), rem(r, 4)
    y, xh, c = div(f, 4), rem(div(f, 2), 2), rem(f, 2)

    def at(yy, xx, cc):
        return (r, yy * 4 + xx * 2 + cc)

    mate, opp, opp_mate = at(y, xh, 1 - c), at(y, 1 - xh, c), at(y, 1 - xh, 1 - c)
    targets = (mate, opp, opp_mate)
    up, down = at(rem(y + 1, 4), xh, c), at(rem(y + 3, 4), xh, c)
    beside = ((1 - xl) * 4 + z, f)
    column = tuple((xl * 4 + rem(z + d, 4), f) for d in (1, 2, 3))

    def send(src, dst, ss, rs, to):
        q = pltpu.make_async_remote_copy(
            src_ref=src, dst_ref=dst, send_sem=ss, recv_sem=rs, device_id=to, device_id_type=MESH
        )
        return q

    def await_bytes(ref, sem):
        pltpu.make_async_copy(ref, ref, sem).wait()

    og_in = pltpu.make_async_copy(og, ogg.at[pl.ds(0, TOK)], ld.at[0])
    og_in.start()
    chunk_order = tuple((s, o) for o in (1, 0) for s in (0, 2, 1, 3))
    loads = {}
    for i, (s, o) in enumerate(chunk_order):
        yy, xx = rem(y + 3 - s + 4, 4), rem(xh + o, 2)
        first = pl.multiple_of((yy * 2 + xx) * (2 * ROWS), 128)
        loads[s, o] = pltpu.make_async_copy(hid.at[:, pl.ds(first, 2 * ROWS)], hv.at[i], ldh.at[i])
        loads[s, o].start()
    state_in = [
        pltpu.make_async_copy(a, b, ld.at[1 + i])
        for i, (a, b) in enumerate(((fm.at[0], fmv), (sm.at[0], smv), (ip.at[0], ipv), (op, opv), (om, omv)))
    ]
    for q in state_in:
        q.start()

    barrier = pltpu.get_barrier_semaphore()
    across = tuple(((1 - xl) * 4 + rem(z + d, 4), f) for d in (1, 2, 3))
    friends = [*targets, up, down, beside, *column] + ([*across] if "d" in GATHER else [])
    for d in friends:
        pl.semaphore_signal(barrier, inc=1, device_id=d, device_id_type=MESH)
    with scope("greet"):
        pl.semaphore_wait(barrier, len(friends))
    with scope("og_in"):
        og_in.wait()

    def part_of(source, k):
        return ogg.at[pl.ds(source * TOK, TOK), pl.ds(k * WIDE, WIDE)]

    og_mate = [send(part_of(0, k), part_of(1, k), ogs, ogm, mate) for k in range(PARTS)]
    og_opp = [send(part_of(0, k), part_of(2, k), ogs, ogx.at[k], opp) for k in range(PARTS)]
    og_pass = [send(part_of(2, k), part_of(3, k), ogs, ogr.at[k], mate) for k in range(PARTS)]
    og_opp[0].start()
    for q in og_mate:
        q.start()

    for i, (s, o) in enumerate(chunk_order):
        with scope(f"turn{i}"):
            loads[s, o].wait()
            turned = hv[i].T
            s_down = (2 - s) % 4
            for cc in range(2):
                for p in range(PIPES):
                    m, off = CUTS[p], OFFS[p]
                    top = turned[ROWS * cc + off : ROWS * cc + off + m]
                    low = turned[ROWS * cc + HALF + off : ROWS * cc + HALF + off + m]
                    if p == OUT:

                        @pl.when(c == cc)
                        def _():
                            hge[s, o * m : (o + 1) * m, 0:TOK] = top
                            hge[s_down, (2 + o) * m : (3 + o) * m, 0:TOK] = low

                        @pl.when(c != cc)
                        def _():
                            hse[s, o * m : (o + 1) * m, :] = top
                            hse[s_down, (2 + o) * m : (3 + o) * m, :] = low

                        continue
                    for t, cond in (((1, c == cc), (2, c != cc)) if o else ((None, c == cc), (0, c != cc))):

                        @pl.when(cond)
                        def _(t=t):
                            if t is None:
                                hg[s, 2 * off : 2 * off + m, 0:TOK] = top
                                hg[s_down, 2 * off + m : 2 * off + 2 * m, 0:TOK] = low
                            else:
                                hs[t, s, 2 * off : 2 * off + m, :] = top
                                hs[t, s_down, 2 * off + m : 2 * off + 2 * m, :] = low

    for s in range(YS):
        send(hse.at[s], hge.at[s, :, pl.ds(TOK, TOK)], hes, her.at[s], mate).start()
    for p, s in LEAVE:
        if p < 0:
            if s:
                og_opp[s].start()
            continue
        rows = pl.ds(2 * OFFS[p], 2 * CUTS[p])
        for t in (1, 2, 0):
            q = send(
                hs.at[t, s, rows],
                hg.at[s, rows, pl.ds(TOK * (t + 1), TOK)],
                hss, hsr.at[p, s], targets[t],
            )
            q.start()

    state_in[2].wait()
    for d in (1, 2, 3):
        there = rem(z + d, 4)
        for side in range(2):
            cols = pl.ds(pl.multiple_of((side * 4 + there) * OWN, OWN), OWN)
            q = send(ipv.at[:, cols], ipr.at[3 - d, side], ips_, ipr_, column[d - 1])
            q.start()

    def sum_inner():
        once("ip", ipr, ipr_)
        with scope("sum_ip"):
            for ref, side in ((ips, 1 - xl), (ipk, xl)):
                cols = pl.ds(pl.multiple_of((side * 4 + z) * OWN, OWN), OWN)
                ref[...] = (ipv[:, cols] + ipr[0, side]) + (ipr[1, side] + ipr[2, side])

    done = set()

    def once(key, ref, sem):
        if key in done:
            return
        done.add(key)
        with scope("w_" + key):
            await_bytes(ref, sem)

    def product(p, s, n, width):
        rows = slice(2 * OFFS[p], 2 * OFFS[p] + 2 * CUTS[p])
        cols = pl.ds(pl.multiple_of(n * width, width), width)
        return rows, cols, jnp.dot(hg[s, rows, :], ogg[:, cols], preferred_element_type=F32)

    def rows_of(p):
        return pl.ds(2 * OFFS[p], 2 * CUTS[p])

    in_parts = set()

    def y_wait(p, s):
        if s == 0 and p in in_parts:
            for k in range(PARTS):
                once(f"y{p}{s}{k}", yrecv.at[s, rows_of(p), pl.ds(k * WIDE, WIDE)], ysp.at[p, k])
        else:
            once(f"y{p}{s}", yrecv.at[s, rows_of(p)], ysr.at[p, s])

    def unit(p, s, part=None):
        m, off = CUTS[p], OFFS[p]
        parts = range(PARTS) if part is None else (part,)
        once(f"hid{p}{s}", hg.at[s, rows_of(p), pl.ds(TOK, 3 * TOK)], hsr.at[p, s])
        for k in parts:
            once(f"og{k}", part_of(3, k), ogr.at[k])
        with scope(f"mm{p}{s}"):

            @pl.loop(parts[0], parts[-1] + 1)
            def _(n):
                rows, cols, got = product(p, s, n, WIDE)
                if s:
                    acc[rows, cols] = got
                else:
                    ysend[s, rows, cols] = got.astype(BF16)

        if s:
            y_wait(p, s - 1)
        if s == 3:
            return
        if s:
            with scope(f"add{p}{s}"):

                @pl.loop(0, REP)
                def _(n):
                    rows, cols = slice(2 * off, 2 * off + 2 * m), pl.ds(pl.multiple_of(n * OWN, OWN), OWN)
                    ysend[s, rows, cols] = (acc[rows, cols] + yrecv[s - 1, rows, cols].astype(F32)).astype(BF16)

        cols = pl.ds(0, COLS) if part is None else pl.ds(part * WIDE, WIDE)
        for start, to in ((2 * off, up), (2 * off + m, down)):
            there = (s, pl.ds(start, m), cols)
            arrived = ysr.at[p, s] if part is None else ysp.at[p, part]
            send(ysend.at[there], yrecv.at[there], yss, arrived, to).start()
        if part is not None:
            in_parts.add(p)

    def out_unit(s):
        m, off = CUTS[OUT], OFFS[OUT]
        once("ogm", ogg.at[pl.ds(TOK, TOK)], ogm)
        once(f"hide{s}", hge.at[s, :, pl.ds(TOK, TOK)], her.at[s])
        with scope(f"mme{s}"):

            @pl.loop(0, PARTS)
            def _(n):
                cols = pl.ds(pl.multiple_of(n * WIDE, WIDE), WIDE)
                got = jnp.dot(hge[s], ogg[0 : 2 * TOK, cols], preferred_element_type=F32)
                if s:
                    ace[:, cols] = got
                else:
                    yse[s, :, cols] = got.astype(BF16)

        if s:
            once(f"ye{s - 1}", yre.at[s - 1], yer.at[s - 1])
            with scope(f"adde{s}"):

                @pl.loop(0, REP)
                def _(n):
                    cols = pl.ds(pl.multiple_of(n * OWN, OWN), OWN)
                    got = ace[:, cols] + yre[s - 1, :, cols].astype(F32)
                    if s < 3:
                        yse[s, :, cols] = got.astype(BF16)
                    else:
                        for i in range(2):
                            acc[2 * off + i * m : 2 * off + (i + 1) * m, cols] = got[2 * i * m : (2 * i + 1) * m]
                            xse[i * m : (i + 1) * m, cols] = got[(2 * i + 1) * m : (2 * i + 2) * m].astype(BF16)

        if s < 3:
            for i, to in enumerate((up, down)):
                there = (s, pl.ds(2 * i * m, 2 * m))
                send(yse.at[there], yre.at[there], yes, yer.at[s], to).start()
        else:
            send(xse, xre, xes, xer, opp).start()

    def adam(p):
        m, off = CUTS[p], OFFS[p]
        if p == OUT:
            once("xe", xre, xer)
        else:
            unit(p, 3)
        if "state" not in done:
            done.add("state")
            for q in (*state_in[:2], *state_in[3:]):
                q.wait()
        with scope(f"adam{p}"):

            @pl.loop(0, REP)
            def _(n):
                cols = pl.ds(pl.multiple_of(n * OWN, OWN), OWN)
                owner_x, owner_z = div(n, 4), rem(n, 4)
                for i, start in enumerate((off, HALF + off)):
                    own_rows, at_rows = slice(2 * off + i * m, 2 * off + (i + 1) * m), slice(start, start + m)
                    last = xre[i * m : (i + 1) * m, cols] if p == OUT else yrecv[2, own_rows, cols]
                    g = acc[own_rows, cols] + last.astype(F32)
                    one = beta_one * fmv[at_rows, cols].astype(F32) + (1.0 - beta_one) * g
                    two = beta_two * smv[at_rows, cols].astype(F32) + (1.0 - beta_two) * g * g
                    fmv[at_rows, cols] = one.astype(BF16)
                    smv[at_rows, cols] = two.astype(BF16)
                    w = ipv[at_rows, cols]
                    hat_one = one * (1.0 / (1.0 - beta_one**INNER_STEP))
                    hat_two = two * (1.0 / (1.0 - beta_two**INNER_STEP))
                    stp[owner_z, owner_x, own_rows, :] = (
                        -inner_rate * (hat_one / (jnp.sqrt(hat_two) + epsilon) + weight_decay * w)
                    ).astype(BF16)

        span = rows_of(p)
        for d in (1, 2, 3):
            there = rem(z + d, 4)
            send(stp.at[there, :, span], rsz.at[3 - d, :, span], rzs, rzr.at[p], column[d - 1]).start()

    def store(a, b, sem):
        pltpu.make_async_copy(a, b, sem).start()

    def reduce_z(p):
        m, off = CUTS[p], OFFS[p]
        rows, span = slice(2 * off, 2 * off + 2 * m), pl.ds(2 * off, 2 * m)
        once(f"rz{p}", rsz.at[:, :, span], rzr.at[p])
        with scope(f"sum{p}"):
            for ref, inner, side in ((xsend, ips, 1 - xl), (xkeep, ipk, xl)):
                a, b, d, e = (
                    v.astype(F32)
                    for v in (stp[z, side, rows, :], rsz[0, side, rows, :], rsz[1, side, rows, :], rsz[2, side, rows, :])
                )
                change = (a + b) + (d + e)
                for i, start in enumerate((off, HALF + off)):
                    ref[2 * off + i * m : 2 * off + (i + 1) * m, :] = (
                        inner[start : start + m, :] + change[i * m : (i + 1) * m]
                    )
        send(xsend.at[span], xrecv.at[span], rxs, rxr.at[p], beside).start()

    def outer(p):
        m, off = CUTS[p], OFFS[p]
        span = pl.ds(2 * off, 2 * m)
        once(f"rx{p}", xrecv.at[span], rxr.at[p])
        with scope(f"outer{p}"):
            for i, start in enumerate((off, HALF + off)):
                own_rows, at_rows = slice(2 * off + i * m, 2 * off + (i + 1) * m), slice(start, start + m)
                params = opv[at_rows, :]
                delta = params - (xkeep[own_rows, :] + xrecv[own_rows, :]) / REP
                momentum = nesterov * omv[at_rows, :] + delta
                omv[at_rows, :] = momentum
                agb[z, xl, own_rows, :] = (params - outer_rate * (delta + nesterov * momentum)).astype(BF16)
        if GATHER[p] == "x":
            give(p, z, xl, axs, axr, beside)
        for to in column:
            give(p, z, xl, azs, azr, to)
        if GATHER[p] != "x":
            give(p, z, xl, axs, axr, beside)
        if GATHER[p] == "d":
            for to in across:
                give(p, z, xl, axs, axr, to)

    def give(p, zz, xx, ss, rs, to):
        here = (zz, xx, rows_of(p))
        send(agb.at[here], agb.at[here], ss, rs.at[p], to).start()

    def pass_on(p):
        if GATHER[p] == "x":
            once(f"ax{p}", agb.at[0, 0, rows_of(p)], axr.at[p])
            for to in column:
                give(p, z, 1 - xl, azs, azr, to)
        else:
            once(f"az{p}", agb.at[pl.ds(0, 3), 0, rows_of(p)], azr.at[p])
            for d in (1, 2, 3):
                give(p, rem(z + d, 4), xl, axs, axr, beside)

    def finish(p):
        m, off = CUTS[p], OFFS[p]
        if GATHER[p] == "x":
            once(f"az{p}", agb.at[pl.ds(0, 3), :, rows_of(p)], azr.at[p])
        else:
            once(f"az{p}", agb.at[pl.ds(0, 3), 0, rows_of(p)], azr.at[p])
            once(f"ax{p}", agb.at[:, 0, rows_of(p)], axr.at[p])
        for zz in range(4):
            for xx in range(2):
                for i, start in enumerate((off, HALF + off)):
                    store(
                        agb.at[zz, xx, pl.ds(2 * off + i * m, m)],
                        o_np.at[pl.ds(start, m), pl.ds((xx * 4 + zz) * OWN, OWN)],
                        stq.at[3],
                    )

    def forward(k):
        once(f"ogx{k}", part_of(2, k), ogx.at[k])
        og_pass[k].start()

    adams, outers = [], []
    run = {
        "out": out_unit, "fwd": forward, "unit": unit, "adam": adam, "rz": reduce_z, "outer": outer,
        "pass": pass_on, "inner": sum_inner, "end": finish,
    }
    for kind, *rest in TASKS:
        run[kind](*rest)
        if kind == "adam":
            adams.append(rest)
            if len(adams) == PIPES:
                store(fmv, o_nf, stq.at[0])
                store(smv, o_ns, stq.at[1])
        if kind == "outer":
            outers.append(rest)
            if len(outers) == PIPES:
                store(omv, o_nm, stq.at[2])

    with scope("drain"):
        await_bytes(ogg.at[pl.ds(0, 3 * TOK)], ogs)
        kept = pl.ds(0, 2 * OFFS[OUT])
        await_bytes(hs.at[:, :, kept], hss)
        await_bytes(ysend.at[:, kept], yss)
        await_bytes(hse, hes)
        await_bytes(yse, yes)
        await_bytes(xse, xes)
        await_bytes(rsz, rzs)
        await_bytes(xsend, rxs)
        for p in range(PIPES):
            x_first = GATHER[p] == "x"
            await_bytes(agb.at[0, 0, rows_of(p)] if x_first else agb.at[:, 0, rows_of(p)], axs)
            await_bytes(agb.at[pl.ds(0, 3), :, rows_of(p)] if x_first else agb.at[pl.ds(0, 3), 0, rows_of(p)], azs)
        await_bytes(ipr, ips_)
        for i, (a, b) in enumerate(((fmv, o_nf), (smv, o_ns), (omv, o_nm))):
            await_bytes(a, stq.at[i])
        await_bytes(fmv, stq.at[3])


def per_device(hidden, out_grad, inner_params, first, second, outer_params, outer_momentum):
    any_ = pl.BlockSpec(memory_space=pl.ANY)
    dma, vmem = pltpu.SemaphoreType.DMA, pltpu.VMEM
    params, momentum, one, two = pl.pallas_call(
        kernel,
        out_shape=(
            jax.ShapeDtypeStruct((ROWS, COLS), BF16),
            jax.ShapeDtypeStruct((ROWS, OWN), F32),
            jax.ShapeDtypeStruct((ROWS, COLS), BF16),
            jax.ShapeDtypeStruct((ROWS, COLS), BF16),
        ),
        in_specs=[any_] * 7,
        out_specs=(any_,) * 4,
        scratch_shapes=[
            vmem((8, TOK, 2 * ROWS), BF16),
            vmem((3, YS, ROWS, TOK), BF16),
            vmem((YS, ROWS, 4 * TOK), BF16),
            vmem((4 * TOK, COLS), BF16),
            vmem((ROWS, COLS), F32),
            vmem((3, ROWS, COLS), BF16),
            vmem((3, ROWS, COLS), BF16),
            vmem((ROWS, COLS), F32),
            vmem((ROWS, COLS), BF16),
            vmem((ROWS, COLS), BF16),
            vmem((ROWS, OWN), F32),
            vmem((ROWS, OWN), F32),
            vmem((4, 2, ROWS, OWN), BF16),
            vmem((3, 2, ROWS, OWN), BF16),
            vmem((ROWS, OWN), F32),
            vmem((ROWS, OWN), F32),
            vmem((ROWS, OWN), F32),
            vmem((4, 2, ROWS, OWN), BF16),
            vmem((3, 2, ROWS, OWN), F32),
            vmem((ROWS, OWN), F32),
            vmem((ROWS, OWN), F32),
            vmem((YS, 4 * CUTS[OUT], TOK), BF16),
            vmem((YS, 4 * CUTS[OUT], 2 * TOK), BF16),
            vmem((4 * CUTS[OUT], COLS), F32),
            vmem((3, 4 * CUTS[OUT], COLS), BF16),
            vmem((3, 4 * CUTS[OUT], COLS), BF16),
            vmem((2 * CUTS[OUT], COLS), BF16),
            vmem((2 * CUTS[OUT], COLS), BF16),
            dma((6,)),
            dma((8,)),
            dma((4,)),
            dma,
            dma,
            dma((PARTS,)),
            dma((PARTS,)),
            dma,
            dma((YS,)),
            dma,
            dma((3,)),
            dma,
            dma,
            dma,
            dma((PIPES, YS)),
            dma,
            dma((PIPES, 3)),
            dma((PIPES, PARTS)),
            dma,
            dma((PIPES,)),
            dma,
            dma((PIPES,)),
            dma,
            dma((PIPES,)),
            dma,
            dma((PIPES,)),
            dma,
            dma,
        ],
        compiler_params=pltpu.CompilerParams(
            collective_id=1, has_side_effects=True, vmem_limit_bytes=60_000_000
        ),
        name="step",
    )(hidden, out_grad, inner_params, first, second, outer_params, outer_momentum)
    return params.astype(F32), momentum, one[None], two[None]


def solution(mesh):
    return jax.shard_map(
        per_device,
        mesh=mesh,
        in_specs=(
            P(("rep", "fsdp"), None),
            P(("rep", "fsdp"), None),
            P("rep", "fsdp", None),
            P("rep", "fsdp", None),
            P("rep", "fsdp", None),
            P("fsdp", "rep"),
            P("fsdp", "rep"),
        ),
        out_specs=(
            P("fsdp", None),
            P("fsdp", "rep"),
            P("rep", "fsdp", None),
            P("rep", "fsdp", None),
        ),
        check_vma=False,
    )
```

time: 305 us -> 117 us (0.38)
  waiting for transfers between devices: 120 us -> 0 us
  blocking collectives: 116 us -> 0 us
  Pallas kernels: 0 us -> 108 us
  matrix products: 19.6 us -> 0 us
  other arithmetic: 22.1 us -> 3.93 us
  between operations: 14.1 us -> 0.66 us
  local copies, waits for them, and re-layouts: 13.1 us -> 4.16 us
    all_gather x2 -> x0, waiting for transfers between devices: 119 us -> none  [the longest x1 74.6 us: per_device(): segment = lax.all_gather(out_grad, 'fsdp', axis=0, tiled=True)]
    all_to_all x2 -> x0, blocking collectives: 116 us -> none  [the longest x1 67.3 us: per_device(): lax.all_to_all(hidden, 'fsdp', split_axis=1, concat_axis=0, tiled=True)]
    pallas_call x0 -> x1, Pallas kernels: none -> 108 us  [per_device(): pl.pallas_call(kernel, out_shape=(jax.ShapeDtypeStruct((ROWS, COLS), BF16...]
    dot_general x1 -> x0, matrix products: 19.6 us -> none  [per_device(): jnp.einsum('btf,btd->bfd', columns.reshape(blocks, token_count, shard_row...]
    reduce_sum x2 -> x0, other arithmetic: 14.7 us -> none  [the longest x1 12.3 us: per_device(): gradient = jnp.sum(rounded, axis=0)]
    unnamed x9, local copies, waits for them, and re-layouts: 11.9 us -> 4.16 us
  transfers between devices with their start and end apart: 2 -> 0, of which waited for: 2 -> 0; matrix products, arithmetic and copies ran while one was open for 2% -> 0% of each run, Pallas kernels for 0% -> 0%
where the time goes in v2:
time: 117 us; the launch traced here: 116 us
  Pallas kernels  108 us (92%)
  local copies, waits for them, and re-layouts  4.16 us (4%)
  other arithmetic  3.93 us (3%)
    pallas_call x1, Pallas kernels, per_device(): pl.pallas_call(kernel, out_shape=(jax.ShapeDtypeStruct((ROWS, COLS), BF16...  108 us
    unnamed x9, local copies, waits for them, and re-layouts  4.16 us
    convert_element_type x1, other arithmetic, per_device(): return (params.astype(F32), momentum, one[None], two[None])  3.93 us

profile of v2, /device:TPU:0, one launch (start us, length us, event | category | flops | bytes accessed | tf_op | source)
XLA Modules:
  0.0 116.4 jit_solution(14788482780296100437)
XLA Ops:
  0.6 107.6 %step.1 = (bf16[448,2048]{1,0:T(8,128)(2,1)}, f32[448,256]{1,0:T(8,128)}, bf16[448,2048]{1,0:T(8,128)(2,1)}, bf16[448,2048]{1,0:T(8,128)(2,1)}) custom-call(bf16[256,7168]{1,0:T(8,128)(2,1)} %hid.1, bf16[256,2048]{1,0:T(8,128)(2,1)} %og.1, f32[1,448,2048]{2,1,0:T(8,128)} %ip.1, bf16[1,448,2048]{2,1,0:T(8,128)(2,1)} %fm.1, bf16[1,448,2048]{2,1,0:T(8,128)(2,1)} %sm.1, ...), custom_call_target="tpu_custom_call" | custom-call | tf_op jit(solution)/shard_map/step/pallas_call | solution.py:442
  108.3 0.0 copy-start.2
  108.3 0.0 copy-start.1
  108.3 3.9 %convert_element_type.3 = f32[448,2048]{1,0:T(8,128)} convert(bf16[448,2048]{1,0:T(8,128)(2,1)} %get-tuple-element.8) | non-fusion elementwise | flops 917504 | bytes 5505024 | tf_op jit(solution)/shard_map/convert_element_type | solution.py:515
  112.2 0.0 copy-done.2
  112.2 0.8 copy.14
  113.0 0.0 copy-done.1
  113.0 0.0 copy-start
  113.0 1.2 %copy.15 = bf16[1,448,2048]{2,1,0:T(8,128)(2,1)} copy(bf16[1,448,2048]{2,1,0:T(8,128)(2,1)S(1)} %bitcast.3) | data formatting | bytes 3670016
  114.2 0.9 copy-done
  115.1 1.2 %copy.16 = bf16[1,448,2048]{2,1,0:T(8,128)(2,1)} copy(bf16[1,448,2048]{2,1,0:T(8,128)(2,1)S(1)} %bitcast.2) | data formatting | bytes 3670016
Async XLA Ops:
  108.3 3.9 %copy-start.2 = (f32[448,256]{1,0:T(8,128)S(1)}, f32[448,256]{1,0:T(8,128)}, u32[]{:S(2)}) copy-start(f32[448,256]{1,0:T(8,128)} %get-tuple-element.17) | copy-start | bytes 1376260
  108.3 4.7 %copy-start.1 = (bf16[448,2048]{1,0:T(8,128)(2,1)S(1)}, bf16[448,2048]{1,0:T(8,128)(2,1)}, u32[]{:S(2)}) copy-start(bf16[448,2048]{1,0:T(8,128)(2,1)} %get-tuple-element.10) | copy-start | bytes 5505028
  113.0 2.2 %copy-start = (bf16[448,2048]{1,0:T(8,128)(2,1)S(1)}, bf16[448,2048]{1,0:T(8,128)(2,1)}, u32[]{:S(2)}) copy-start(bf16[448,2048]{1,0:T(8,128)(2,1)} %get-tuple-element.11) | copy-start | bytes 5505028

commit v3 on v2

--- a/solution.py
+++ b/solution.py
@@ -20,7 +20,7 @@
 MESH = pl.DeviceIdType.MESH
 BF16, F32 = jnp.bfloat16, jnp.float32
 
-CUTS = (64, 64, 16, 32, 16, 32)
+CUTS = (48, 48, 32, 16, 48, 32)
 OUT = 5
 OFFS = tuple(sum(CUTS[:p]) for p in range(len(CUTS)))
 PIPES = len(CUTS)
@@ -30,21 +30,21 @@
 PARTS = 4
 WIDE = COLS // PARTS
 LEAVE = (
-    (-1, 0), (0, 0), (1, 0), (2, 0), (-1, 1), (-1, 2), (-1, 3), (3, 0), (4, 0), (0, 1), (1, 1), (2, 1), (3, 1),
-    (4, 1), (0, 2), (1, 2), (2, 2), (3, 2), (4, 2), (0, 3), (1, 3), (2, 3), (3, 3), (4, 3),
+    (-1, 0), (2, 0), (1, 0), (-1, 1), (0, 0), (-1, 2), (-1, 3), (2, 1), (4, 0), (3, 0), (0, 1), (3, 1), (1, 1),
+    (2, 3), (0, 2), (1, 2), (0, 3), (4, 1), (4, 2), (2, 2), (1, 3), (3, 3), (3, 2), (4, 3),
 )
 TASKS = (
-    ("out", 0), ("fwd", 0), ("unit", 0, 0, 0), ("out", 1), ("unit", 2, 0, 0), ("fwd", 1), ("unit", 1, 0, 0),
-    ("out", 2), ("unit", 1, 0, 1), ("fwd", 2), ("unit", 1, 0, 2), ("unit", 0, 0, 2), ("unit", 0, 0, 1),
-    ("unit", 2, 0, 2), ("fwd", 3), ("out", 3), ("unit", 2, 0, 1), ("unit", 2, 0, 3), ("unit", 0, 0, 3),
-    ("unit", 1, 0, 3), ("unit", 3, 0), ("unit", 0, 1), ("unit", 4, 0), ("unit", 1, 1), ("unit", 0, 2),
-    ("unit", 3, 1), ("unit", 1, 2), ("adam", 0), ("unit", 4, 1), ("unit", 2, 1), ("inner",), ("adam", 5),
-    ("unit", 3, 2), ("adam", 1), ("unit", 4, 2), ("rz", 0), ("unit", 2, 2), ("adam", 3), ("rz", 5), ("adam", 4),
-    ("adam", 2), ("rz", 1), ("outer", 0), ("rz", 3), ("rz", 4), ("outer", 5), ("rz", 2), ("outer", 1), ("outer", 3),
-    ("outer", 2), ("pass", 5), ("outer", 4), ("pass", 0), ("pass", 1), ("pass", 2), ("pass", 3), ("pass", 4),
-    ("end", 1), ("end", 4), ("end", 3), ("end", 5), ("end", 0), ("end", 2),
+    ("out", 0), ("fwd", 0), ("unit", 1, 0, 0), ("out", 1), ("fwd", 1), ("unit", 2, 0, 1), ("unit", 1, 0, 1),
+    ("out", 2), ("unit", 0, 0, 0), ("fwd", 2), ("unit", 0, 0, 2), ("unit", 2, 0, 0), ("unit", 0, 0, 1),
+    ("unit", 1, 0, 2), ("unit", 2, 0, 2), ("fwd", 3), ("unit", 2, 0, 3), ("unit", 1, 0, 3), ("unit", 0, 0, 3),
+    ("unit", 4, 0), ("unit", 0, 1), ("unit", 1, 1), ("unit", 0, 2), ("out", 3), ("unit", 1, 2), ("unit", 4, 1),
+    ("inner",), ("unit", 2, 1), ("adam", 0), ("adam", 1), ("unit", 4, 2), ("rz", 0), ("unit", 3, 0), ("adam", 5),
+    ("unit", 2, 2), ("rz", 1), ("outer", 0), ("adam", 4), ("unit", 3, 1), ("adam", 2), ("rz", 5), ("unit", 3, 2),
+    ("outer", 1), ("rz", 4), ("outer", 5), ("adam", 3), ("pass", 0), ("rz", 2), ("outer", 4), ("pass", 1),
+    ("rz", 3), ("outer", 2), ("end", 1), ("outer", 3), ("pass", 5), ("end", 0), ("pass", 4), ("end", 2), ("end", 3),
+    ("end", 5), ("end", 4),
 )
-GATHER = "zxxzzx"
+GATHER = "xzddxz"
 
 
 def rem(a, b):
@@ -60,7 +60,7 @@
     o_np, o_nm, o_nf, o_ns,
     hv, hs, hg, ogg, acc, ysend, yrecv, ipv, fmv, smv, opv, omv, stp, rsz, xsend, xkeep, xrecv, agb,
     ipr, ips, ipk, hse, hge, ace, yse, yre, xse, xre,
-    ld, ldh, stq, ogs, ogm, ogx, ogr, hes, her, yes, yer, xes, xer,
+    ld, ldh, ogs, ogm, ogx, ogr, hes, her, yes, yer, xes, xer,
     hss, hsr, yss, ysr, ysp, rzs, rzr, rxs, rxr, axs, axr, azs, azr,
     ips_, ipr_,
 ):
@@ -309,8 +309,8 @@
                     g = acc[own_rows, cols] + last.astype(F32)
                     one = beta_one * fmv[at_rows, cols].astype(F32) + (1.0 - beta_one) * g
                     two = beta_two * smv[at_rows, cols].astype(F32) + (1.0 - beta_two) * g * g
-                    fmv[at_rows, cols] = one.astype(BF16)
-                    smv[at_rows, cols] = two.astype(BF16)
+                    o_nf[at_rows, cols] = one.astype(BF16)
+                    o_ns[at_rows, cols] = two.astype(BF16)
                     w = ipv[at_rows, cols]
                     hat_one = one * (1.0 / (1.0 - beta_one**INNER_STEP))
                     hat_two = two * (1.0 / (1.0 - beta_two**INNER_STEP))
@@ -322,9 +322,6 @@
         for d in (1, 2, 3):
             there = rem(z + d, 4)
             send(stp.at[there, :, span], rsz.at[3 - d, :, span], rzs, rzr.at[p], column[d - 1]).start()
-
-    def store(a, b, sem):
-        pltpu.make_async_copy(a, b, sem).start()
 
     def reduce_z(p):
         m, off = CUTS[p], OFFS[p]
@@ -353,7 +350,7 @@
                 params = opv[at_rows, :]
                 delta = params - (xkeep[own_rows, :] + xrecv[own_rows, :]) / REP
                 momentum = nesterov * omv[at_rows, :] + delta
-                omv[at_rows, :] = momentum
+                o_nm[at_rows, :] = momentum
                 agb[z, xl, own_rows, :] = (params - outer_rate * (delta + nesterov * momentum)).astype(BF16)
         if GATHER[p] == "x":
             give(p, z, xl, axs, axr, beside)
@@ -386,35 +383,24 @@
         else:
             once(f"az{p}", agb.at[pl.ds(0, 3), 0, rows_of(p)], azr.at[p])
             once(f"ax{p}", agb.at[:, 0, rows_of(p)], axr.at[p])
-        for zz in range(4):
-            for xx in range(2):
-                for i, start in enumerate((off, HALF + off)):
-                    store(
-                        agb.at[zz, xx, pl.ds(2 * off + i * m, m)],
-                        o_np.at[pl.ds(start, m), pl.ds((xx * 4 + zz) * OWN, OWN)],
-                        stq.at[3],
-                    )
+        with scope(f"out{p}"):
+            for zz in range(4):
+                for xx in range(2):
+                    for i, start in enumerate((off, HALF + off)):
+                        o_np[start : start + m, (xx * 4 + zz) * OWN : (xx * 4 + zz + 1) * OWN] = agb[
+                            zz, xx, 2 * off + i * m : 2 * off + (i + 1) * m, :
+                        ]
 
     def forward(k):
         once(f"ogx{k}", part_of(2, k), ogx.at[k])
         og_pass[k].start()
 
-    adams, outers = [], []
     run = {
         "out": out_unit, "fwd": forward, "unit": unit, "adam": adam, "rz": reduce_z, "outer": outer,
         "pass": pass_on, "inner": sum_inner, "end": finish,
     }
     for kind, *rest in TASKS:
         run[kind](*rest)
-        if kind == "adam":
-            adams.append(rest)
-            if len(adams) == PIPES:
-                store(fmv, o_nf, stq.at[0])
-                store(smv, o_ns, stq.at[1])
-        if kind == "outer":
-            outers.append(rest)
-            if len(outers) == PIPES:
-                store(omv, o_nm, stq.at[2])
 
     with scope("drain"):
         await_bytes(ogg.at[pl.ds(0, 3 * TOK)], ogs)
@@ -431,9 +417,6 @@
             await_bytes(agb.at[0, 0, rows_of(p)] if x_first else agb.at[:, 0, rows_of(p)], axs)
             await_bytes(agb.at[pl.ds(0, 3), :, rows_of(p)] if x_first else agb.at[pl.ds(0, 3), 0, rows_of(p)], azs)
         await_bytes(ipr, ips_)
-        for i, (a, b) in enumerate(((fmv, o_nf), (smv, o_ns), (omv, o_nm))):
-            await_bytes(a, stq.at[i])
-        await_bytes(fmv, stq.at[3])
 
 
 def per_device(hidden, out_grad, inner_params, first, second, outer_params, outer_momentum):
@@ -442,13 +425,13 @@
     params, momentum, one, two = pl.pallas_call(
         kernel,
         out_shape=(
-            jax.ShapeDtypeStruct((ROWS, COLS), BF16),
-            jax.ShapeDtypeStruct((ROWS, OWN), F32),
-            jax.ShapeDtypeStruct((ROWS, COLS), BF16),
-            jax.ShapeDtypeStruct((ROWS, COLS), BF16),
+            vmem((ROWS, COLS), BF16),
+            vmem((ROWS, OWN), F32),
+            vmem((ROWS, COLS), BF16),
+            vmem((ROWS, COLS), BF16),
         ),
         in_specs=[any_] * 7,
-        out_specs=(any_,) * 4,
+        out_specs=(pl.BlockSpec(memory_space=vmem),) * 4,
         scratch_shapes=[
             vmem((8, TOK, 2 * ROWS), BF16),
             vmem((3, YS, ROWS, TOK), BF16),
@@ -480,7 +463,6 @@
             vmem((2 * CUTS[OUT], COLS), BF16),
             dma((6,)),
             dma((8,)),
-            dma((4,)),
             dma,
             dma,
             dma((PARTS,)),
@@ -508,7 +490,7 @@
             dma,
         ],
         compiler_params=pltpu.CompilerParams(
-            collective_id=1, has_side_effects=True, vmem_limit_bytes=60_000_000
+            collective_id=1, has_side_effects=True, vmem_limit_bytes=55_000_000
         ),
         name="step",
     )(hidden, out_grad, inner_params, first, second, outer_params, outer_momentum)

time: 117 us -> 112 us (0.957)
  Pallas kernels: 108 us -> 105 us
  other arithmetic: 3.93 us -> 2.28 us
    pallas_call x1, Pallas kernels: 108 us -> 105 us  [per_device(): pl.pallas_call(kernel, out_shape=(vmem((ROWS, COLS), BF16), vmem((ROWS, O...]
    convert_element_type x1, other arithmetic: 3.93 us -> 2.28 us  [per_device(): return (params.astype(F32), momentum, one[None], two[None])]
    unnamed x9 -> x3, local copies, waits for them, and re-layouts: 4.16 us -> 3.23 us
where the time goes in v3:
time: 112 us; the launch traced here: 111 us
  Pallas kernels  105 us (94%)
  local copies, waits for them, and re-layouts  3.23 us (3%)
  other arithmetic  2.28 us (2%)
    pallas_call x1, Pallas kernels, per_device(): pl.pallas_call(kernel, out_shape=(vmem((ROWS, COLS), BF16), vmem((ROWS, O...  105 us
    unnamed x3, local copies, waits for them, and re-layouts  3.23 us
    convert_element_type x1, other arithmetic, per_device(): return (params.astype(F32), momentum, one[None], two[None])  2.28 us

profile of v3, /device:TPU:0, one launch (start us, length us, event | category | flops | bytes accessed | tf_op | source)
XLA Modules:
  0.0 111.1 jit_solution(5090860108562887806)
XLA Ops:
  0.6 105.0 %step.1 = (bf16[448,2048]{1,0:T(8,128)(2,1)S(1)}, f32[448,256]{1,0:T(8,128)S(1)}, bf16[448,2048]{1,0:T(8,128)(2,1)S(1)}, bf16[448,2048]{1,0:T(8,128)(2,1)S(1)}) custom-call(bf16[256,7168]{1,0:T(8,128)(2,1)} %hid.1, bf16[256,2048]{1,0:T(8,128)(2,1)} %og.1, f32[1,448,2048]{2,1,0:T(8,128)} %ip.1, bf16[1,448,2048]{2,1,0:T(8,128)(2,1)} %fm.1, ...), custom_call_target="tpu_custom_call" | custom-call | tf_op jit(solution)/shard_map/step/pallas_call | solution.py:425
  105.6 0.8 copy.14
  106.4 2.3 %convert_element_type.3 = f32[448,2048]{1,0:T(8,128)} convert(bf16[448,2048]{1,0:T(8,128)(2,1)S(1)} %get-tuple-element.8) | non-fusion elementwise | flops 917504 | bytes 5505024 | tf_op jit(solution)/shard_map/convert_element_type | solution.py:497
  108.7 1.2 %copy.15 = bf16[1,448,2048]{2,1,0:T(8,128)(2,1)} copy(bf16[1,448,2048]{2,1,0:T(8,128)(2,1)S(1)} %bitcast.3) | data formatting | bytes 3670016
  109.9 1.2 %copy.16 = bf16[1,448,2048]{2,1,0:T(8,128)(2,1)} copy(bf16[1,448,2048]{2,1,0:T(8,128)(2,1)S(1)} %bitcast.2) | data formatting | bytes 3670016

commit v4 on v3

--- a/solution.py
+++ b/solution.py
@@ -89,7 +89,7 @@
 
     og_in = pltpu.make_async_copy(og, ogg.at[pl.ds(0, TOK)], ld.at[0])
     og_in.start()
-    chunk_order = tuple((s, o) for o in (1, 0) for s in (0, 2, 1, 3))
+    chunk_order = ((0, 1), (2, 1), (0, 0), (2, 0), (1, 1), (3, 1), (1, 0), (3, 0))
     loads = {}
     for i, (s, o) in enumerate(chunk_order):
         yy, xx = rem(y + 3 - s + 4, 4), rem(xh + o, 2)
@@ -108,22 +108,14 @@
     friends = [*targets, up, down, beside, *column] + ([*across] if "d" in GATHER else [])
     for d in friends:
         pl.semaphore_signal(barrier, inc=1, device_id=d, device_id_type=MESH)
-    with scope("greet"):
-        pl.semaphore_wait(barrier, len(friends))
-    with scope("og_in"):
-        og_in.wait()
-
     def part_of(source, k):
         return ogg.at[pl.ds(source * TOK, TOK), pl.ds(k * WIDE, WIDE)]
 
     og_mate = [send(part_of(0, k), part_of(1, k), ogs, ogm, mate) for k in range(PARTS)]
     og_opp = [send(part_of(0, k), part_of(2, k), ogs, ogx.at[k], opp) for k in range(PARTS)]
     og_pass = [send(part_of(2, k), part_of(3, k), ogs, ogr.at[k], mate) for k in range(PARTS)]
-    og_opp[0].start()
-    for q in og_mate:
-        q.start()
-
-    for i, (s, o) in enumerate(chunk_order):
+    def turn(i):
+        s, o = chunk_order[i]
         with scope(f"turn{i}"):
             loads[s, o].wait()
             turned = hv[i].T
@@ -157,21 +149,38 @@
                                 hs[t, s, 2 * off : 2 * off + m, :] = top
                                 hs[t, s_down, 2 * off + m : 2 * off + 2 * m, :] = low
 
-    for s in range(YS):
-        send(hse.at[s], hge.at[s, :, pl.ds(TOK, TOK)], hes, her.at[s], mate).start()
-    for p, s in LEAVE:
+    for i in range(4):
+        turn(i)
+    with scope("greet"):
+        pl.semaphore_wait(barrier, len(friends))
+    with scope("og_in"):
+        og_in.wait()
+    og_opp[0].start()
+    out_hid = [send(hse.at[s], hge.at[s, :, pl.ds(TOK, TOK)], hes, her.at[s], mate) for s in range(YS)]
+    out_hid[0].start()
+    for q in og_mate:
+        q.start()
+
+    def leave(p, s):
         if p < 0:
             if s:
                 og_opp[s].start()
-            continue
+            return
         rows = pl.ds(2 * OFFS[p], 2 * CUTS[p])
         for t in (1, 2, 0):
-            q = send(
-                hs.at[t, s, rows],
-                hg.at[s, rows, pl.ds(TOK * (t + 1), TOK)],
-                hss, hsr.at[p, s], targets[t],
-            )
-            q.start()
+            send(
+                hs.at[t, s, rows], hg.at[s, rows, pl.ds(TOK * (t + 1), TOK)], hss, hsr.at[p, s], targets[t]
+            ).start()
+
+    ahead = next(i for i, (p, s) in enumerate(LEAVE) if p >= 0 and s % 2)
+    for p, s in LEAVE[:ahead]:
+        leave(p, s)
+    for i in range(4, 8):
+        turn(i)
+    for q in out_hid[1:]:
+        q.start()
+    for p, s in LEAVE[ahead:]:
+        leave(p, s)
 
     state_in[2].wait()
     for d in (1, 2, 3):
@@ -419,6 +428,26 @@
         await_bytes(ipr, ips_)
 
 
+SLABS = 7
+
+
+def write_out(params, momentum, one, two, o_params, o_momentum, o_one, o_two, wide, sem):
+    copies = [
+        pltpu.make_async_copy(a, b, sem.at[i])
+        for i, (a, b) in enumerate(((one, o_one), (two, o_two), (momentum, o_momentum)))
+    ]
+    for q in copies:
+        q.start()
+    for k in range(SLABS):
+        rows = pl.ds(k * (ROWS // SLABS), ROWS // SLABS)
+        wide[rows, :] = params[rows, :].astype(F32)
+        q = pltpu.make_async_copy(wide.at[rows], o_params.at[rows], sem.at[3 + k])
+        q.start()
+        copies.append(q)
+    for q in copies:
+        q.wait()
+
+
 def per_device(hidden, out_grad, inner_params, first, second, outer_params, outer_momentum):
     any_ = pl.BlockSpec(memory_space=pl.ANY)
     dma, vmem = pltpu.SemaphoreType.DMA, pltpu.VMEM
@@ -494,7 +523,21 @@
         ),
         name="step",
     )(hidden, out_grad, inner_params, first, second, outer_params, outer_momentum)
-    return params.astype(F32), momentum, one[None], two[None]
+    params, momentum, one, two = pl.pallas_call(
+        write_out,
+        out_shape=(
+            jax.ShapeDtypeStruct((ROWS, COLS), F32),
+            jax.ShapeDtypeStruct((ROWS, OWN), F32),
+            jax.ShapeDtypeStruct((ROWS, COLS), BF16),
+            jax.ShapeDtypeStruct((ROWS, COLS), BF16),
+        ),
+        in_specs=[pl.BlockSpec(memory_space=vmem)] * 4,
+        out_specs=(any_,) * 4,
+        scratch_shapes=[vmem((ROWS, COLS), F32), dma((3 + SLABS,))],
+        compiler_params=pltpu.CompilerParams(vmem_limit_bytes=8_000_000),
+        name="write",
+    )(params, momentum, one, two)
+    return params, momentum, one[None], two[None]
 
 
 def solution(mesh):

time: 112 us -> 109 us (0.973)
  local copies, waits for them, and re-layouts: 3.23 us -> 0 us
  Pallas kernels: 105 us -> 108 us
  other arithmetic: 2.28 us -> 0 us
    unnamed x3 -> x0, local copies, waits for them, and re-layouts: 3.23 us -> none
    pallas_call x0 -> x1, Pallas kernels: none -> 3.2 us  [per_device(): pl.pallas_call(write_out, out_shape=(jax.ShapeDtypeStruct((ROWS, COLS), F...]
    convert_element_type x1 -> x0, other arithmetic: 2.28 us -> none  [per_device(): return (params.astype(F32), momentum, one[None], two[None])]
where the time goes in v4:
time: 109 us
  Pallas kernels  108 us (99%)
    pallas_call x1, Pallas kernels, per_device(): pl.pallas_call(kernel, out_shape=(vmem((ROWS, COLS), BF16), vmem((ROWS, O...  105 us
    pallas_call x1, Pallas kernels, per_device(): pl.pallas_call(write_out, out_shape=(jax.ShapeDtypeStruct((ROWS, COLS), F...  3.2 us

profile of v4, /device:TPU:0, one launch (start us, length us, event | category | flops | bytes accessed | tf_op | source)
XLA Modules:
  0.0 108.7 jit_solution(17102995903013304910)
XLA Ops:
  0.6 104.9 %step.1 = (bf16[448,2048]{1,0:T(8,128)(2,1)S(1)}, f32[448,256]{1,0:T(8,128)S(1)}, bf16[448,2048]{1,0:T(8,128)(2,1)S(1)}, bf16[448,2048]{1,0:T(8,128)(2,1)S(1)}) custom-call(bf16[256,7168]{1,0:T(8,128)(2,1)} %hid.1, bf16[256,2048]{1,0:T(8,128)(2,1)} %og.1, f32[1,448,2048]{2,1,0:T(8,128)} %ip.1, bf16[1,448,2048]{2,1,0:T(8,128)(2,1)} %fm.1, ...), custom_call_target="tpu_custom_call" | custom-call | tf_op jit(solution)/shard_map/step/pallas_call | solution.py:454
  105.5 3.2 %write.1 = (f32[448,2048]{1,0:T(8,128)}, f32[448,256]{1,0:T(8,128)}, bf16[448,2048]{1,0:T(8,128)(2,1)}, bf16[448,2048]{1,0:T(8,128)(2,1)}) custom-call(bf16[448,2048]{1,0:T(8,128)(2,1)S(1)} %get-tuple-element.12.params, f32[448,256]{1,0:T(8,128)S(1)} %get-tuple-element.13.momentum, bf16[448,2048]{1,0:T(8,128)(2,1)S(1)} %get-tuple-element.14.one, ...), custom_call_target="tpu_custom_call" | custom-call | tf_op jit(solution)/shard_map/write/pallas_call | solution.py:526

commit v5 on v4

--- a/solution.py
+++ b/solution.py
@@ -40,10 +40,10 @@
     ("unit", 4, 0), ("unit", 0, 1), ("unit", 1, 1), ("unit", 0, 2), ("out", 3), ("unit", 1, 2), ("unit", 4, 1),
     ("inner",), ("unit", 2, 1), ("adam", 0), ("adam", 1), ("unit", 4, 2), ("rz", 0), ("unit", 3, 0), ("adam", 5),
     ("unit", 2, 2), ("rz", 1), ("outer", 0), ("adam", 4), ("unit", 3, 1), ("adam", 2), ("rz", 5), ("unit", 3, 2),
-    ("outer", 1), ("rz", 4), ("outer", 5), ("adam", 3), ("pass", 0), ("rz", 2), ("outer", 4), ("pass", 1),
-    ("rz", 3), ("outer", 2), ("end", 1), ("outer", 3), ("pass", 5), ("end", 0), ("pass", 4), ("end", 2), ("end", 3),
-    ("end", 5), ("end", 4),
+    ("outer", 1), ("outer", 5), ("adam", 3), ("pass", 0), ("rz", 2), ("outer", 4), ("pass", 1), ("outer", 2),
+    ("end", 1), ("outer", 3), ("pass", 5), ("end", 0), ("pass", 4), ("end", 2), ("end", 3), ("end", 5), ("end", 4),
 )
+SUM = "zzzddz"
 GATHER = "xzddxz"
 
 
@@ -59,10 +59,10 @@
     hid, og, ip, fm, sm, op, om,
     o_np, o_nm, o_nf, o_ns,
     hv, hs, hg, ogg, acc, ysend, yrecv, ipv, fmv, smv, opv, omv, stp, rsz, xsend, xkeep, xrecv, agb,
-    ipr, ips, ipk, hse, hge, ace, yse, yre, xse, xre,
+    ipr, ips, ipk, ipx, xrb, hse, hge, ace, yse, yre, xse, xre,
     ld, ldh, ogs, ogm, ogx, ogr, hes, her, yes, yer, xes, xer,
     hss, hsr, yss, ysr, ysp, rzs, rzr, rxs, rxr, axs, axr, azs, azr,
-    ips_, ipr_,
+    ips_, ipr_, ixs, ixr,
 ):
     scope = jax.named_scope
     r, f = lax.axis_index("rep"), lax.axis_index("fsdp")
@@ -105,7 +105,7 @@
 
     barrier = pltpu.get_barrier_semaphore()
     across = tuple(((1 - xl) * 4 + rem(z + d, 4), f) for d in (1, 2, 3))
-    friends = [*targets, up, down, beside, *column] + ([*across] if "d" in GATHER else [])
+    friends = [*targets, up, down, beside, *column] + ([*across] if "d" in SUM + GATHER else [])
     for d in friends:
         pl.semaphore_signal(barrier, inc=1, device_id=d, device_id_type=MESH)
     def part_of(source, k):
@@ -196,6 +196,11 @@
             for ref, side in ((ips, 1 - xl), (ipk, xl)):
                 cols = pl.ds(pl.multiple_of((side * 4 + z) * OWN, OWN), OWN)
                 ref[...] = (ipv[:, cols] + ipr[0, side]) + (ipr[1, side] + ipr[2, side])
+        for p in range(PIPES):
+            if SUM[p] == "d":
+                for start in (OFFS[p], HALF + OFFS[p]):
+                    rows = pl.ds(start, CUTS[p])
+                    send(ips.at[rows], ipx.at[rows], ixs, ixr.at[p], beside).start()
 
     done = set()
 
@@ -330,7 +335,13 @@
         span = rows_of(p)
         for d in (1, 2, 3):
             there = rem(z + d, 4)
-            send(stp.at[there, :, span], rsz.at[3 - d, :, span], rzs, rzr.at[p], column[d - 1]).start()
+            if SUM[p] == "z":
+                send(stp.at[there, :, span], rsz.at[3 - d, :, span], rzs, rzr.at[p], column[d - 1]).start()
+            else:
+                send(stp.at[there, xl, span], rsz.at[3 - d, 0, span], rzs, rzr.at[p], column[d - 1]).start()
+                send(stp.at[there, 1 - xl, span], rsz.at[3 - d, 1, span], rzs, rzr.at[p], across[d - 1]).start()
+        if SUM[p] == "d":
+            send(stp.at[z, 1 - xl, span], xrb.at[span], rxs, rxr.at[p], beside).start()
 
     def reduce_z(p):
         m, off = CUTS[p], OFFS[p]
@@ -352,12 +363,24 @@
     def outer(p):
         m, off = CUTS[p], OFFS[p]
         span = pl.ds(2 * off, 2 * m)
-        once(f"rx{p}", xrecv.at[span], rxr.at[p])
+        if SUM[p] == "z":
+            once(f"rx{p}", xrecv.at[span], rxr.at[p])
+        else:
+            once(f"rz{p}", rsz.at[:, :, span], rzr.at[p])
+            once(f"rx{p}", xrb.at[span], rxr.at[p])
+            once(f"ix{p}", ipx.at[span], ixr.at[p])
         with scope(f"outer{p}"):
             for i, start in enumerate((off, HALF + off)):
                 own_rows, at_rows = slice(2 * off + i * m, 2 * off + (i + 1) * m), slice(start, start + m)
                 params = opv[at_rows, :]
-                delta = params - (xkeep[own_rows, :] + xrecv[own_rows, :]) / REP
+                if SUM[p] == "z":
+                    total = xkeep[own_rows, :] + xrecv[own_rows, :]
+                else:
+                    change = stp[z, xl, own_rows, :].astype(F32) + xrb[own_rows, :].astype(F32)
+                    for k in range(3):
+                        change = change + (rsz[k, 0, own_rows, :].astype(F32) + rsz[k, 1, own_rows, :].astype(F32))
+                    total = (ipk[at_rows, :] + ipx[at_rows, :]) + change
+                delta = params - total / REP
                 momentum = nesterov * omv[at_rows, :] + delta
                 o_nm[at_rows, :] = momentum
                 agb[z, xl, own_rows, :] = (params - outer_rate * (delta + nesterov * momentum)).astype(BF16)
@@ -420,7 +443,10 @@
         await_bytes(yse, yes)
         await_bytes(xse, xes)
         await_bytes(rsz, rzs)
-        await_bytes(xsend, rxs)
+        for p in range(PIPES):
+            await_bytes((xsend if SUM[p] == "z" else xrb).at[rows_of(p)], rxs)
+            if SUM[p] == "d":
+                await_bytes(ipx.at[rows_of(p)], ixs)
         for p in range(PIPES):
             x_first = GATHER[p] == "x"
             await_bytes(agb.at[0, 0, rows_of(p)] if x_first else agb.at[:, 0, rows_of(p)], axs)
@@ -428,7 +454,7 @@
         await_bytes(ipr, ips_)
 
 
-SLABS = 7
+SLABS = 14
 
 
 def write_out(params, momentum, one, two, o_params, o_momentum, o_one, o_two, wide, sem):
@@ -483,6 +509,8 @@
             vmem((3, 2, ROWS, OWN), F32),
             vmem((ROWS, OWN), F32),
             vmem((ROWS, OWN), F32),
+            vmem((ROWS, OWN), F32),
+            vmem((ROWS, OWN), BF16),
             vmem((YS, 4 * CUTS[OUT], TOK), BF16),
             vmem((YS, 4 * CUTS[OUT], 2 * TOK), BF16),
             vmem((4 * CUTS[OUT], COLS), F32),
@@ -517,6 +545,8 @@
             dma((PIPES,)),
             dma,
             dma,
+            dma,
+            dma((PIPES,)),
         ],
         compiler_params=pltpu.CompilerParams(
             collective_id=1, has_side_effects=True, vmem_limit_bytes=55_000_000

time: 109 us -> 109 us (level)
  no operation moved by 1% of the time
where the time goes in v5:
time: 109 us
  Pallas kernels  108 us (99%)
    pallas_call x1, Pallas kernels, per_device(): pl.pallas_call(kernel, out_shape=(vmem((ROWS, COLS), BF16), vmem((ROWS, O...  105 us
    pallas_call x1, Pallas kernels, per_device(): pl.pallas_call(write_out, out_shape=(jax.ShapeDtypeStruct((ROWS, COLS), F...  3.24 us

profile of v5, /device:TPU:0, one launch (start us, length us, event | category | flops | bytes accessed | tf_op | source)
XLA Modules:
  0.0 108.6 jit_solution(15661637165268333385)
XLA Ops:
  0.6 104.8 %step.1 = (bf16[448,2048]{1,0:T(8,128)(2,1)S(1)}, f32[448,256]{1,0:T(8,128)S(1)}, bf16[448,2048]{1,0:T(8,128)(2,1)S(1)}, bf16[448,2048]{1,0:T(8,128)(2,1)S(1)}) custom-call(bf16[256,7168]{1,0:T(8,128)(2,1)} %hid.1, bf16[256,2048]{1,0:T(8,128)(2,1)} %og.1, f32[1,448,2048]{2,1,0:T(8,128)} %ip.1, bf16[1,448,2048]{2,1,0:T(8,128)(2,1)} %fm.1, ...), custom_call_target="tpu_custom_call" | custom-call | tf_op jit(solution)/shard_map/step/pallas_call | solution.py:480
  105.4 3.2 %write.1 = (f32[448,2048]{1,0:T(8,128)}, f32[448,256]{1,0:T(8,128)}, bf16[448,2048]{1,0:T(8,128)(2,1)}, bf16[448,2048]{1,0:T(8,128)(2,1)}) custom-call(bf16[448,2048]{1,0:T(8,128)(2,1)S(1)} %get-tuple-element.12.params, f32[448,256]{1,0:T(8,128)S(1)} %get-tuple-element.13.momentum, bf16[448,2048]{1,0:T(8,128)(2,1)S(1)} %get-tuple-element.14.one, ...), custom_call_target="tpu_custom_call" | custom-call | tf_op jit(solution)/shard_map/write/pallas_call | solution.py:556
